TPU v7x, 32 devices: a whole 2x2x4 slice. The times are simulated.
32 devices in a mesh: tm: 16 (over z, x, core), space: 2 (over y).
Axes of the slice: x: 2, y: 2, z: 4, core: 2. Of those that a mesh axis runs over, the one named last changes fastest.
Arguments:
- forcing: float32 [16, 8, 128, 128], P('tm', 'space'), may hold values from -6 to 6
- initial: float32 [8, 128, 128], P('space'), may hold values from -6 to 6
- coupling: float32 [8, 128, 128], P('space'), may hold values from 0.3 to 3
- velocity: float32 [3, 8, 128, 128], P(None, 'space'), may hold values from -0.9 to 0.9
Outputs:
- iterate: float32 [16, 8, 128, 128], P('tm', 'space')
All inputs are finite; a program needn't handle non-finite values.
Results may differ from a plain program's by a relative error of at most 0.0003.
Values sent between devices are 32-bit elements; how exact they have to be, the bound alone decides.
A program may use at most 64 MiB of HBM per device.

v0:
```python
import math

import jax
import jax.numpy as jnp
import numpy as np
from jax import lax
from jax.experimental import pallas as pl
from jax.experimental.pallas import tpu as pltpu
from jax.sharding import PartitionSpec as P

ITERS = 2
SWEEPS = 8
HALO = 8

wrap_alpha = 0.1


def forward_table(steps):
    n = np.arange(steps)
    gamma = wrap_alpha ** (n / steps)
    table = np.zeros((steps // 2, 2, steps))
    for u in range(steps // 2):
        angle = 2.0 * np.pi * ((u * n) % steps) / steps
        if u == 0:
            table[u, 0] = gamma
            table[u, 1] = (1.0 - 2.0 * (n % 2)) * gamma
        else:
            table[u, 0] = np.cos(angle) * gamma
            table[u, 1] = -np.sin(angle) * gamma
    return table


def inverse_table(steps):
    n = np.arange(steps)
    table = np.zeros((steps // 2, 2, steps))
    for u in range(steps // 2):
        angle = 2.0 * np.pi * ((u * n) % steps) / steps
        if u == 0:
            table[u, 0] = 1.0 / steps
            table[u, 1] = (1.0 - 2.0 * (n % 2)) / steps
        else:
            table[u, 0] = 2.0 * np.cos(angle) / steps
            table[u, 1] = -2.0 * np.sin(angle) / steps
    return table


def by_index(index, values):
    picked = jnp.float32(values[0])
    for at in range(1, len(values)):
        picked = jnp.where(index == at, jnp.float32(values[at]), picked)
    return picked


def kernel(
    dims,
    f_ref,
    k_ref,
    out_ref,
    times,
    fields,
    edge,
    kbuf,
    coef,
    pq,
    src,
    wa,
    wb,
    whalo,
    part,
    gathered,
    reduced,
    last,
    back,
    states,
    s1,
    r1,
    s2,
    r2,
    sk,
    rk,
    sf,
    rf,
    se,
    re,
    sw,
    rw,
    ss,
    rs,
    sg,
    rg,
    s3,
    r3,
    s4,
    r4,
):
    T, S, NY, NX, zl = dims
    U = T // 2
    NZ = zl * S
    C = zl * NY // T
    bands = 2 * S
    R = NY // bands
    RH = R + 2 * HALO
    q = C // R
    planes = NZ // U
    rho = wrap_alpha ** (1.0 / T)
    forward = forward_table(T)
    inverse = inverse_table(T)
    n = np.arange(T)
    gamma = wrap_alpha ** (n / T)

    t = lax.axis_index("tm")
    s = lax.axis_index("space")
    group = t // zl
    zi = t % zl
    unit = (zi * S + s) // q
    band = group * q + (zi * S + s) % q
    row0 = pl.multiple_of(group * C, 8)

    def place(u, b):
        at = u * q + b % q
        return (b // q) * zl + at // S, at % S

    def chunk(tt):
        start = (tt % zl) * NY + (tt // zl) * C
        return pl.ds(pl.multiple_of(start, 8), C)

    ring = range(1, T)

    def device(tt, ts):
        return {"tm": tt, "space": ts}

    def remote(source, target, ssem, rsem, tt, ts):
        return pltpu.make_async_remote_copy(
            src_ref=source,
            dst_ref=target,
            send_sem=ssem,
            recv_sem=rsem,
            device_id=device(tt, ts),
            device_id_type=pl.DeviceIdType.MESH,
        )

    barrier = pltpu.get_barrier_semaphore()
    for d in range(1, T):
        pl.semaphore_signal(barrier, inc=1, device_id=device(lax.rem(t + d, T), s), device_id_type=pl.DeviceIdType.MESH)
    for d in range(1, S):
        pl.semaphore_signal(barrier, inc=1, device_id=device(t, lax.rem(s + d, S)), device_id_type=pl.DeviceIdType.MESH)
    pl.semaphore_wait(barrier, T + S - 2)
    sent = []

    def send(source, target, ssem, rsem, tt, ts, valid=None, maybe_self=True):
        copy = remote(source, target, ssem, rsem, tt, ts)
        same = jnp.logical_and(tt == t, ts == s) if maybe_self else None
        away = valid
        if maybe_self:
            here = same if valid is None else jnp.logical_and(valid, same)
            away = jnp.logical_not(same)
            if valid is not None:
                away = jnp.logical_and(valid, away)

            @pl.when(here)
            def _():
                pltpu.make_async_copy(source, target, rsem).start()

        if away is None:
            copy.start()
            sent.append(copy.wait_send)
        else:

            @pl.when(away)
            def _():
                copy.start()

            def finish():
                @pl.when(away)
                def _():
                    copy.wait_send()

            sent.append(finish)

    def arrived(target, rsem, valid=None):
        if valid is None:
            pltpu.make_async_copy(target, target, rsem).wait()
        else:

            @pl.when(valid)
            def _():
                pltpu.make_async_copy(target, target, rsem).wait()

    for d in ring:
        tt = lax.rem(t + d, T)
        send(
            f_ref.at[chunk(tt)],
            times.at[t],
            s1.at[d],
            r1.at[d],
            tt,
            s,
            maybe_self=False,
        )
    send(
        k_ref.at[4, zl - 1, pl.ds(row0 + HALO, C)],
        edge.at[0],
        se.at[0],
        re.at[0],
        t,
        jnp.minimum(s + 1, S - 1),
        valid=s + 1 < S,
        maybe_self=False,
    )
    send(
        k_ref.at[4, 0, pl.ds(row0 + HALO, C)],
        edge.at[1],
        se.at[1],
        re.at[1],
        t,
        jnp.maximum(s - 1, 0),
        valid=s > 0,
        maybe_self=False,
    )
    half = zl // 2
    share = (t % 2) * half
    rest = half - share
    partner = t + 1 - 2 * (t % 2)
    for d in range(1, S):
        ts = lax.rem(s + d, S)
        rows = pl.ds(pl.multiple_of((group * q + (zi * S + ts) % q) * R, 8), RH)
        source = k_ref.at[pl.ds(0, 4), pl.ds(share, half), rows]
        target = kbuf.at[:, pl.ds(s * zl + share, half)]
        send(source, target, sk.at[d], rk.at[d], t, ts, maybe_self=False)
    times[pl.ds(t, 1)] = f_ref[chunk(t)][None]

    angles = [2.0 * math.pi * u / U / 2 for u in range(U)]
    shift_re1 = by_index(unit, [rho * math.cos(a) for a in angles])
    shift_im1 = by_index(unit, [0.0] + [rho * math.sin(a) for a in angles[1:]])
    shift_re2 = by_index(unit, [-rho] + [rho * math.cos(a) for a in angles[1:]])
    wide_column = lax.broadcasted_iota(jnp.int32, (RH, NX), 1)

    def prepare(z, c, vz, vy, vx):
        az = c * vz
        ay = c * vy
        ax = c * vx
        zero = jnp.zeros_like(c)
        coef[0, z] = jnp.where(z == NZ - 1, zero, c - az)
        coef[1, z] = jnp.where(z == 0, zero, c + az)
        coef[2, z] = c - ay
        coef[3, z] = c + ay
        coef[4, z] = jnp.where(wide_column == NX - 1, zero, c - ax)
        coef[5, z] = jnp.where(wide_column == 0, zero, c + ax)
        diag1 = 1.0 + 6.0 * c - shift_re1
        diag2 = 1.0 + 6.0 * c - shift_re2
        im2 = shift_im1 * shift_im1
        modulus1 = diag1 * diag1 + im2
        modulus2 = diag2 * diag2 + im2
        pq[0, z] = diag1 / modulus1
        pq[1, z] = diag2 / modulus2
        pq[2, z] = shift_im1 / modulus1

    band_rows = pl.ds(pl.multiple_of(band * R, 8), RH)
    for o in range(zl):
        prepare(s * zl + o, *[k_ref[m, o, band_rows] for m in range(4)])

    def shifted(value, by, axis):
        return pltpu.roll(value, by % value.shape[axis], axis)

    window = pl.ds(row0, C + 2 * HALO)
    inner = pl.ds(row0 + HALO, C)
    column = lax.broadcasted_iota(jnp.int32, (C, NX), 1)
    arrived(edge.at[0], re.at[0], valid=s > 0)
    arrived(edge.at[1], re.at[1], valid=s + 1 < S)

    @pl.when(s == 0)
    def _():
        edge[0] = jnp.zeros((C, NX), jnp.float32)

    @pl.when(s + 1 == S)
    def _():
        edge[1] = jnp.zeros((C, NX), jnp.float32)

    wide = k_ref[4, zi, window]
    middle = wide[HALO : HALO + C]
    lower = jnp.where(zi == 0, edge[0], k_ref[4, jnp.maximum(zi - 1, 0), inner])
    upper = jnp.where(zi == zl - 1, edge[1], k_ref[4, jnp.minimum(zi + 1, zl - 1), inner])
    coupling = k_ref[0, zi, inner]
    adz = coupling * k_ref[1, zi, inner]
    ady = coupling * k_ref[2, zi, inner]
    adx = coupling * k_ref[3, zi, inner]
    summed = (coupling - adz) * upper + (coupling + adz) * lower
    summed += (coupling - ady) * shifted(wide, -1, 0)[HALO : HALO + C]
    summed += (coupling + ady) * shifted(wide, 1, 0)[HALO : HALO + C]
    summed += (coupling - adx) * jnp.where(column == NX - 1, 0.0, shifted(middle, -1, 1))
    summed += (coupling + adx) * jnp.where(column == 0, 0.0, shifted(middle, 1, 1))
    start = summed - 6.0 * coupling * middle

    for d in range(1, T):
        arrived(times.at[lax.rem(t + T - d, T)], r1.at[d])

    for block in range(C // 8):
        rows = slice(block * 8, block * 8 + 8)
        values = [times[m, rows] + start[rows] for m in range(T)]
        for u in range(U):
            for p in range(2):
                total = values[0] * float(forward[u, p, 0])
                for m in range(1, T):
                    total = total + values[m] * float(forward[u, p, m])
                fields[u, p, rows] = total

    z = s * zl + zi
    for step in range(U):
        u = lax.rem(unit + step, U)
        for o in range(q):
            b = group * q + o
            for kind in range(3):
                to = b + (0, -1, 1)[kind]
                valid = (None, to >= 0, to < bands)[kind]
                safe = jnp.clip(to, 0, bands - 1)
                first, count, land = (
                    (o * R, R, HALO),
                    (o * R, HALO, HALO + R),
                    (o * R + R - HALO, HALO, 0),
                )[kind]
                to_t, to_s = place(u, safe)
                send(
                    fields.at[u, :, pl.ds(first, count)],
                    src.at[:, z, pl.ds(land, count)],
                    s2.at[step, o, kind],
                    r2.at[z, kind],
                    to_t,
                    to_s,
                    valid=valid,
                )

    for d in range(1, S):
        theirs = lax.rem(s + S - d, S) * zl
        block = kbuf.at[:, pl.ds(theirs + share, half)]
        arrived(block, rk.at[d])
        send(block, block, sf.at[d], rf.at[d], partner, s, maybe_self=False)
    for d in range(1, S):
        theirs = lax.rem(s + S - d, S) * zl
        for o in range(half):
            at = theirs + share + o
            prepare(at, *[kbuf[m, at] for m in range(4)])
        arrived(kbuf.at[:, pl.ds(theirs + rest, half)], rf.at[d])
        for o in range(half):
            at = theirs + rest + o
            prepare(at, *[kbuf[m, at] for m in range(4)])

    @pl.when(band == 0)
    def _():
        src[:, :, :HALO] = jnp.zeros((2, NZ, HALO, NX), jnp.float32)
        last[:, :HALO] = jnp.zeros((NZ, HALO, NX), jnp.float32)
        whalo[0] = jnp.zeros((2, NZ, HALO, NX), jnp.float32)

    @pl.when(band == bands - 1)
    def _():
        src[:, :, HALO + R :] = jnp.zeros((2, NZ, HALO, NX), jnp.float32)
        last[:, HALO + R :] = jnp.zeros((NZ, HALO, NX), jnp.float32)
        whalo[1] = jnp.zeros((2, NZ, HALO, NX), jnp.float32)

    for z in range(NZ):
        arrived(src.at[:, z, pl.ds(HALO, R)], r2.at[z, 0])
        arrived(src.at[:, z, pl.ds(HALO + R, HALO)], r2.at[z, 1], valid=band < bands - 1)
        arrived(src.at[:, z, pl.ds(0, HALO)], r2.at[z, 2], valid=band > 0)

    def scale(z, re_part, im_part, target):
        p1, p2, im = pq[0, z], pq[1, z], pq[2, z]
        target[0, z] = re_part * p1 + im_part * im
        target[1, z] = im_part * p2 - re_part * im

    together = math.gcd(NZ, 8)

    def sweep(old, new):
        @pl.loop(0, NZ // together)
        def _(trip):
            for o in range(together):
                z = trip * together + o
                up = jnp.minimum(z + 1, NZ - 1) if o == together - 1 else z + 1
                down = jnp.maximum(z - 1, 0) if o == 0 else z - 1
                sums = []
                for p in range(2):
                    here = old[p, z]
                    total = src[p, z] + coef[0, z] * old[p, up] + coef[1, z] * old[p, down]
                    total += coef[2, z] * shifted(here, -1, 0) + coef[3, z] * shifted(here, 1, 0)
                    total += coef[4, z] * shifted(here, -1, 1) + coef[5, z] * shifted(here, 1, 1)
                    sums.append(total)
                scale(z, sums[0], sums[1], new)

    @pl.loop(0, NZ)
    def _(z):
        scale(z, src[0, z], src[1, z], wa)

    @pl.loop(0, SWEEPS // 2)
    def _(i):
        sweep(wa, wb)
        sweep(wb, wa)

    below = jnp.maximum(band - 1, 0)
    above = jnp.minimum(band + 1, bands - 1)
    send(
        wa.at[:, :, pl.ds(HALO + R - HALO, HALO)],
        whalo.at[0],
        sw.at[0],
        rw.at[0],
        *place(unit, above),
        valid=band < bands - 1,
        maybe_self=False,
    )
    send(
        wa.at[:, :, pl.ds(HALO, HALO)],
        whalo.at[1],
        sw.at[1],
        rw.at[1],
        *place(unit, below),
        valid=band > 0,
        maybe_self=False,
    )
    weight_re = by_index(unit, [float(inverse[u, 0, T - 1]) for u in range(U)])
    weight_im = by_index(unit, [float(inverse[u, 1, T - 1]) for u in range(U)])

    @pl.loop(0, NZ)
    def _(z):
        part[z] = weight_re * wa[0, z, HALO : HALO + R] + weight_im * wa[1, z, HALO : HALO + R]

    for d in range(1, U):
        u = lax.rem(unit + d, U)
        send(
            part.at[pl.ds(u * planes, planes)],
            gathered.at[unit],
            ss.at[d],
            rs.at[d],
            *place(u, band),
            maybe_self=False,
        )
    gathered[pl.ds(unit, 1)] = part[pl.ds(unit * planes, planes)][None]
    for d in range(1, U):
        arrived(gathered.at[lax.rem(unit + U - d, U)], rs.at[d])
    total = gathered[0]
    for u in range(1, U):
        total = total + gathered[u]
    reduced[...] = total * rho
    mine = pl.ds(unit * planes, planes)
    for d in range(U):
        u = lax.rem(unit + d, U)
        for kind in range(3):
            to = band + (0, -1, 1)[kind]
            valid = (None, to >= 0, to < bands)[kind]
            safe = jnp.clip(to, 0, bands - 1)
            first, count, land = ((0, R, HALO), (0, HALO, HALO + R), (R - HALO, HALO, 0))[kind]
            if kind == 0 and d == 0:
                last[mine, HALO : HALO + R] = reduced[...]
                continue
            send(
                reduced.at[:, pl.ds(first, count)],
                last.at[mine, pl.ds(land, count)],
                sg.at[d, kind],
                rg.at[d, kind],
                *place(u, safe),
                valid=valid,
                maybe_self=False,
            )
    arrived(whalo.at[0], rw.at[0], valid=band > 0)
    arrived(whalo.at[1], rw.at[1], valid=band < bands - 1)
    sent_before = list(sent)
    sent.clear()
    for finish in sent_before:
        finish()
    wa[:, :, :HALO] = whalo[0]
    wa[:, :, HALO + R :] = whalo[1]
    for d in range(U):
        theirs = pl.ds(lax.rem(unit + U - d, U) * planes, planes)
        if d:
            arrived(last.at[theirs, pl.ds(HALO, R)], rg.at[d, 0])
        arrived(last.at[theirs, pl.ds(HALO + R, HALO)], rg.at[d, 1], valid=band < bands - 1)
        arrived(last.at[theirs, pl.ds(0, HALO)], rg.at[d, 2], valid=band > 0)

    @pl.loop(0, NZ)
    def _(z):
        src[0, z] = src[0, z] - last[z]
        src[1, z] = src[1, z] - jnp.where(unit == 0, last[z], jnp.zeros_like(last[z]))

    @pl.loop(0, SWEEPS // 2)
    def _(i):
        sweep(wa, wb)
        sweep(wb, wa)

    sweep(wa, wb)

    for step in range(NZ):
        z = lax.rem(unit * planes + step, NZ)
        at = group * zl + z % zl
        offset = pl.multiple_of((band % q) * R, 8)
        send(
            wb.at[:, z, pl.ds(HALO, R)],
            back.at[unit, :, pl.ds(offset, R)],
            s3.at[step],
            r3.at[unit, lax.rem(band, q)],
            at,
            z // zl,
        )
    for u in range(U):
        for o in range(q):
            arrived(back.at[u, :, pl.ds(o * R, R)], r3.at[u, o])
    for block in range(C // 8):
        rows = slice(block * 8, block * 8 + 8)
        values = [back[u, p, rows] for u in range(U) for p in range(2)]
        begin = middle[rows]
        for m in range(T):
            total = begin
            for at in range(T):
                total = total + values[at] * float(inverse[at // 2, at % 2, m] / gamma[m])
            states[m, rows] = total
    for d in ring:
        tt = lax.rem(t + d, T)
        send(
            states.at[tt],
            out_ref.at[chunk(t)],
            s4.at[d],
            r4.at[d],
            tt,
            s,
            maybe_self=False,
        )
    out_ref[chunk(t)] = states[pl.ds(t, 1)][0]
    for d in range(1, T):
        tt = lax.rem(t + T - d, T)
        arrived(out_ref.at[chunk(tt)], r4.at[d])
    for finish in sent:
        finish()


def body(forcing, initial, coupling, velocity):
    local_steps, zl, NY, NX = forcing.shape
    T = lax.axis_size("tm")
    S = lax.axis_size("space")
    U = T // 2
    NZ = zl * S
    C = zl * NY // T
    bands = 2 * S
    R = NY // bands
    RH = R + 2 * HALO
    q = C // R
    planes = NZ // U
    assert local_steps == 1 and SWEEPS <= HALO <= R and ITERS == 2
    assert S % q == 0 and zl % 2 == 0 and T % 2 == 0
    assert C % R == 0 and NY % C == 0 and NZ % U == 0
    stacked = jnp.concatenate([coupling[None], velocity, initial[None]], axis=0)
    stacked = jnp.pad(stacked, ((0, 0), (0, 0), (HALO, HALO), (0, 0)))
    f32 = jnp.float32
    dma = pltpu.SemaphoreType.DMA
    out = pl.pallas_call(
        lambda *refs: kernel((T, S, NY, NX, zl), *refs),
        out_shape=jax.ShapeDtypeStruct((zl * NY, NX), f32),
        in_specs=[pl.BlockSpec(memory_space=pltpu.VMEM)] * 2,
        out_specs=pl.BlockSpec(memory_space=pltpu.VMEM),
        scratch_shapes=[
            pltpu.VMEM((T, C, NX), f32),
            pltpu.VMEM((U, 2, C, NX), f32),
            pltpu.VMEM((2, C, NX), f32),
            pltpu.VMEM((4, NZ, RH, NX), f32),
            pltpu.VMEM((6, NZ, RH, NX), f32),
            pltpu.VMEM((3, NZ, RH, NX), f32),
            pltpu.VMEM((2, NZ, RH, NX), f32),
            pltpu.VMEM((2, NZ, RH, NX), f32),
            pltpu.VMEM((2, NZ, RH, NX), f32),
            pltpu.VMEM((2, 2, NZ, HALO, NX), f32),
            pltpu.VMEM((NZ, R, NX), f32),
            pltpu.VMEM((U, planes, R, NX), f32),
            pltpu.VMEM((planes, R, NX), f32),
            pltpu.VMEM((NZ, RH, NX), f32),
            pltpu.VMEM((U, 2, C, NX), f32),
            pltpu.VMEM((T, C, NX), f32),
            dma((T,)),
            dma((T,)),
            dma((U, q, 3)),
            dma((NZ, 3)),
            dma((S,)),
            dma((S,)),
            dma((S,)),
            dma((S,)),
            dma((2,)),
            dma((2,)),
            dma((2,)),
            dma((2,)),
            dma((U,)),
            dma((U,)),
            dma((U, 3)),
            dma((U, 3)),
            dma((NZ,)),
            dma((U, q)),
            dma((T,)),
            dma((T,)),
        ],
        compiler_params=pltpu.CompilerParams(
            has_side_effects=True, collective_id=0, vmem_limit_bytes=48 * 1024 * 1024
        ),
    )(forcing.reshape(zl * NY, NX), stacked)
    return out.reshape(forcing.shape)


def solution(mesh):
    return jax.shard_map(
        body,
        mesh=mesh,
        in_specs=(
            P("tm", "space", None, None),
            P("space", None, None),
            P("space", None, None),
            P(None, "space", None, None),
        ),
        out_specs=P("tm", "space", None, None),
        check_vma=False,
    )
```

profile of v0, /device:TPU:1, one launch (start us, length us, event | category | flops | bytes accessed | tf_op | source)
XLA Modules:
  0.0 47.1 jit_solution(7756467580331032594)
XLA Ops:
  0.0 0.0 copy-start
  0.0 1.4 %select_maximum_fusion.refs_1_ = f32[5,4,144,128]{3,2,1,0:T(8,128)S(1)} fusion(f32[1,4,128,128]{3,2,1,0:T(8,128)} %bitcast.6, f32[3,4,128,128]{3,2,1,0:T(8,128)} %param.7, f32[1,4,128,128]{3,2,1,0:T(8,128)} %bitcast.7), kind=kLoop, calls=%fused_computation.2 | loop fusion | flops 2949120 | bytes 2785280 | tf_op jit(solution)/shard_map/concatenate | solution.py:545
  1.4 0.0 copy-done
  1.4 45.0 %shard_map.46 = f32[512,128]{1,0:T(8,128)S(1)} custom-call(f32[512,128]{1,0:T(8,128)S(1)} %bitcast.5, f32[5,4,144,128]{3,2,1,0:T(8,128)S(1)} %select_maximum_fusion.refs_1_), custom_call_target="tpu_custom_call" | custom-call | tf_op jit(solution)/shard_map/pallas_call | solution.py:549
  46.4 0.7 %copy.6 = f32[1,4,128,128]{3,2,1,0:T(8,128)} copy(f32[1,4,128,128]{3,2,1,0:T(8,128)S(1)} %bitcast.4) | data formatting | bytes 524288
Async XLA Ops:
  0.0 1.4 %copy-start = (f32[1,4,128,128]{3,2,1,0:T(8,128)S(1)}, f32[1,4,128,128]{3,2,1,0:T(8,128)}, u32[]{:S(2)}) copy-start(f32[1,4,128,128]{3,2,1,0:T(8,128)} %param.4) | copy-start | bytes 786436
where the time goes:
time: 47.3 us; the launch traced here: 47.1 us
  Pallas kernels  45 us (95%)
  other arithmetic  1.42 us (3%)
  local copies, waits for them, and re-layouts  0.71 us (2%)
    pallas_call x1, Pallas kernels, body(): pl.pallas_call(lambda *refs: kernel((T, S, NY, NX, zl), *refs), out_shape...  45 us
    concatenate x1, other arithmetic, body(): stacked = jnp.concatenate([coupling[None], velocity, initial[None]], axis=0)  1.42 us

commit v1 on v0

v1 whole, which is shorter than its diff:
```python
import math

import jax
import jax.numpy as jnp
import numpy as np
from jax import lax
from jax.experimental import pallas as pl
from jax.experimental.pallas import tpu as pltpu
from jax.sharding import PartitionSpec as P

ITERS = 2
SWEEPS = 8
HALO = 8
GUARD = SWEEPS + 1

wrap_alpha = 0.1


def by_index(index, values):
    picked = jnp.float32(values[0])
    for at in range(1, len(values)):
        picked = jnp.where(index == at, jnp.float32(values[at]), picked)
    return picked


def weighted(terms):
    total = None
    for weight, value in terms:
        if abs(weight) < 1e-12:
            continue
        if abs(weight - 1.0) < 1e-12:
            term = value
        elif abs(weight + 1.0) < 1e-12:
            term = None
            total = -value if total is None else total - value
        else:
            term = value * float(weight)
        if term is not None:
            total = term if total is None else total + term
    return total


def plus(first, second):
    return second if first is None else first if second is None else first + second


def minus(first, second):
    return first if second is None else -second if first is None else first - second


def forward_transform(values):
    T = len(values)
    U = T // 2
    gamma = [wrap_alpha ** (n / T) for n in range(T)]
    a = [values[n] if n == 0 else values[n] * float(gamma[n]) for n in range(T)]
    even = {n: a[n] + a[T - n] for n in range(1, U)}
    odd = {n: a[n] - a[T - n] for n in range(1, U)}

    def cosine(u, parity):
        return weighted([(math.cos(2 * math.pi * u * n / T), even[n]) for n in range(1, U) if n % 2 == parity])

    def sine(u, parity):
        return weighted([(math.sin(2 * math.pi * u * n / T), odd[n]) for n in range(1, U) if n % 2 == parity])

    result = [None] * U
    ends = [a[0] + a[U], a[0] - a[U]]
    zero_even = plus(ends[0], cosine(0, 0))
    zero_odd = cosine(0, 1)
    result[0] = (plus(zero_even, zero_odd), minus(zero_even, zero_odd))
    for u in range(1, U // 2 + 1):
        c_even = plus(ends[u % 2], cosine(u, 0))
        c_odd = cosine(u, 1)
        s_even, s_odd = sine(u, 0), sine(u, 1)
        if u == U - u:
            result[u] = (plus(c_even, c_odd), minus(None, plus(s_even, s_odd)))
            continue
        result[u] = (plus(c_even, c_odd), minus(None, plus(s_even, s_odd)))
        result[U - u] = (minus(c_even, c_odd), minus(s_even, s_odd))
    return result


def inverse_transform(pairs, begin):
    U = len(pairs)
    T = 2 * U
    scale = [1.0 / (T * wrap_alpha ** (m / T)) for m in range(T)]
    first, middle = pairs[0]
    ends = [first + middle, first - middle]

    def cosine(m, parity):
        return weighted([(2 * math.cos(2 * math.pi * u * m / T), pairs[u][0]) for u in range(1, U) if u % 2 == parity])

    def sine(m, parity):
        return weighted([(2 * math.sin(2 * math.pi * u * m / T), pairs[u][1]) for u in range(1, U) if u % 2 == parity])

    result = [None] * T

    def put(m, real, imaginary):
        for at, value in ((m, minus(real, imaginary)), ((T - m) % T, plus(real, imaginary))):
            if result[at] is None:
                result[at] = begin + value * float(scale[at])

    for m in range(0, U // 2 + 1):
        c_even, c_odd = plus(ends[m % 2], cosine(m, 0)), cosine(m, 1)
        s_even, s_odd = sine(m, 0), sine(m, 1)
        put(m, plus(c_even, c_odd), plus(s_even, s_odd))
        other = U - m
        if other != m:
            put(other, minus(c_even, c_odd), minus(s_odd, s_even))
    return result


def kernel(
    dims,
    f_hbm,
    i_hbm,
    c_hbm,
    v_hbm,
    out_ref,
    fbuf,
    ini,
    kc,
    times,
    fields,
    edge,
    kin,
    coef,
    pq,
    land,
    src,
    wa,
    wb,
    wc,
    part,
    gathered,
    reduced,
    last,
    fin,
    back,
    states,
    sl,
    s1,
    r1,
    s2,
    r2,
    sk,
    rk,
    sf,
    rf,
    se,
    re,
    sw,
    rw,
    ss,
    rs,
    sg,
    rg,
    s3,
    r3,
    s4,
    r4,
):
    T, S, NY, NX, zl = dims
    U = T // 2
    NZ = zl * S
    C = zl * NY // T
    bands = 2 * S
    R = NY // bands
    RH = R + 2 * HALO
    WC = C + 2 * HALO
    q = C // R
    PK = RH + 3 * HALO
    PS = RH + HALO
    PF = R + HALO
    chunk_rows = R * NZ // U
    edges = HALO * U // R
    rho = wrap_alpha ** (1.0 / T)
    O = GUARD

    t = lax.axis_index("tm")
    s = lax.axis_index("space")
    group = t // zl
    zi = t % zl
    at = zi * S + s
    unit = at // q
    band = group * q + at % q
    plane = s * zl + zi
    row0 = pl.multiple_of(group * C, 8)

    def place(u, b):
        spot = u * q + b % q
        return (b // q) * zl + spot // S, spot % S

    def chunk(tt):
        start = (tt % zl) * NY + (tt // zl) * C
        return pl.ds(pl.multiple_of(start, 8), C)

    def device(tt, ts):
        return {"tm": tt, "space": ts}

    def remote(source, target, ssem, rsem, tt, ts):
        return pltpu.make_async_remote_copy(
            src_ref=source,
            dst_ref=target,
            send_sem=ssem,
            recv_sem=rsem,
            device_id=device(tt, ts),
            device_id_type=pl.DeviceIdType.MESH,
        )

    barrier = pltpu.get_barrier_semaphore()
    for m in range(T - 1, 0, -1):
        pl.semaphore_signal(barrier, inc=1, device_id=device(t ^ m, s), device_id_type=pl.DeviceIdType.MESH)
    for m in range(1, S):
        pl.semaphore_signal(barrier, inc=1, device_id=device(t, s ^ m), device_id_type=pl.DeviceIdType.MESH)

    def window(start, count):
        first = jnp.clip(start - HALO, 0, NY - count)
        offset = HALO + first - (start - HALO)
        return pl.ds(pl.multiple_of(first, 8), count), pl.ds(pl.multiple_of(offset, 8), count)

    def space_window(ts):
        return window((group * q + (zi * S + ts) % q) * R, RH)

    own = pl.ds(s * zl, zl)
    k_from, k_to = space_window(s)
    i_from, i_to = window(row0, WC)
    local = [
        pltpu.make_async_copy(f_hbm, fbuf, sl.at[0]),
        pltpu.make_async_copy(i_hbm.at[:, i_from], ini.at[:, i_to], sl.at[1]),
        pltpu.make_async_copy(c_hbm.at[zi, pl.ds(row0, C)], kc.at[0], sl.at[2]),
        pltpu.make_async_copy(v_hbm.at[:, zi, pl.ds(row0, C)], kc.at[pl.ds(1, 3)], sl.at[3]),
        pltpu.make_async_copy(c_hbm.at[:, k_from], kin.at[0, own, k_to], sl.at[4]),
        pltpu.make_async_copy(v_hbm.at[:, :, k_from], kin.at[pl.ds(1, 3), own, k_to], sl.at[5]),
    ]
    for copy in local:
        copy.start()

    @pl.when(group == 0)
    def _():
        ini[:, HALO : 2 * HALO] = jnp.zeros((zl, HALO, NX), jnp.float32)

    @pl.when(row0 + C == NY)
    def _():
        ini[:, WC : WC + HALO] = jnp.zeros((zl, HALO, NX), jnp.float32)

    @pl.when(band == 0)
    def _():
        kin[:, :, HALO : 2 * HALO] = jnp.zeros((4, NZ, HALO, NX), jnp.float32)

    @pl.when(band == bands - 1)
    def _():
        kin[:, :, RH : RH + HALO] = jnp.zeros((4, NZ, HALO, NX), jnp.float32)

    pl.semaphore_wait(barrier, T + S - 2)
    sent = []

    def send(source, target, ssem, rsem, tt, ts, valid=None, maybe_self=False):
        copy = remote(source, target, ssem, rsem, tt, ts)
        away = valid
        if maybe_self:
            same = jnp.logical_and(tt == t, ts == s)
            here = same if valid is None else jnp.logical_and(valid, same)
            away = jnp.logical_not(same)
            if valid is not None:
                away = jnp.logical_and(valid, away)

            @pl.when(here)
            def _():
                pltpu.make_async_copy(source, target, rsem).start()

        if away is None:
            copy.start()
            sent.append(copy.wait_send)
        else:

            @pl.when(away)
            def _():
                copy.start()

            def finish():
                @pl.when(away)
                def _():
                    copy.wait_send()

            sent.append(finish)

    def arrived(target, rsem, valid=None):
        if valid is None:
            pltpu.make_async_copy(target, target, rsem).wait()
        else:

            @pl.when(valid)
            def _():
                pltpu.make_async_copy(target, target, rsem).wait()

    local[0].wait()
    for m in range(T - 1, 0, -1):
        tt = t ^ m
        send(fbuf.at[chunk(tt)], times.at[t], s1.at[m], r1.at[m], tt, s)
    inner_rows = pl.ds(row0, C)
    up_s = jnp.minimum(s + 1, S - 1)
    down_s = jnp.maximum(s - 1, 0)
    send(i_hbm.at[zl - 1, inner_rows], edge.at[0], se.at[0], re.at[0], t, up_s, valid=s + 1 < S)
    send(i_hbm.at[0, inner_rows], edge.at[1], se.at[1], re.at[1], t, down_s, valid=s > 0)
    half = zl // 2
    share = (t % 2) * half
    rest = half - share
    partner = t ^ 1
    for m in range(1, S):
        ts = s ^ m
        from_rows, to_rows = space_window(ts)
        give = pl.ds(share, half)
        put = pl.ds(s * zl + share, half)
        send(c_hbm.at[give, from_rows], kin.at[0, put, to_rows], sk.at[m, 0], rk.at[m, 0], t, ts)
        send(v_hbm.at[:, give, from_rows], kin.at[pl.ds(1, 3), put, to_rows], sk.at[m, 1], rk.at[m, 1], t, ts)
    times[pl.ds(t, 1)] = fbuf[chunk(t)][None]
    for copy in local[1:]:
        copy.wait()

    def shifted(value, by, axis):
        return pltpu.roll(value, by % value.shape[axis], axis)

    column = lax.broadcasted_iota(jnp.int32, (C, NX), 1)
    arrived(edge.at[0], re.at[0], valid=s > 0)
    arrived(edge.at[1], re.at[1], valid=s + 1 < S)

    @pl.when(s == 0)
    def _():
        edge[0] = jnp.zeros((C, NX), jnp.float32)

    @pl.when(s + 1 == S)
    def _():
        edge[1] = jnp.zeros((C, NX), jnp.float32)

    inner = pl.ds(2 * HALO, C)
    wide = ini[zi, pl.ds(HALO, WC)]
    middle = wide[HALO : HALO + C]
    lower = jnp.where(zi == 0, edge[0], ini[jnp.maximum(zi - 1, 0), inner])
    upper = jnp.where(zi == zl - 1, edge[1], ini[jnp.minimum(zi + 1, zl - 1), inner])
    coupling = kc[0]
    adz = coupling * kc[1]
    ady = coupling * kc[2]
    adx = coupling * kc[3]
    summed = (coupling - adz) * upper + (coupling + adz) * lower
    summed += (coupling - ady) * shifted(wide, -1, 0)[HALO : HALO + C]
    summed += (coupling + ady) * shifted(wide, 1, 0)[HALO : HALO + C]
    summed += (coupling - adx) * jnp.where(column == NX - 1, 0.0, shifted(middle, -1, 1))
    summed += (coupling + adx) * jnp.where(column == 0, 0.0, shifted(middle, 1, 1))
    start = summed - 6.0 * coupling * middle

    for m in range(1, T):
        arrived(times.at[t ^ m], r1.at[m])

    for block in range(C // 8):
        rows = slice(block * 8, block * 8 + 8)
        spectrum = forward_transform([times[m, rows] + start[rows] for m in range(T)])
        for u in range(U):
            for p in range(2):
                fields[u, p, rows] = spectrum[u][p]

    kinds = ((0, R, HALO), (0, HALO, HALO + R), (R - HALO, HALO, 0))

    def lying(z, first, count):
        return land.at[:, pl.ds(pl.multiple_of(z * PS + first, 8), count)]

    for m in range(NZ - 1, -1, -1):
        spot = at ^ m
        u = spot // q
        o = spot % q
        b = group * q + o
        for kind in range(3):
            to = b + (0, -1, 1)[kind]
            valid = (None, to >= 0, to < bands)[kind]
            first, count, put = kinds[kind]
            source = fields.at[u, :, pl.ds(pl.multiple_of(o * R + first, 8), count)]
            if kind == 0 and m == 0:
                own_rows = pl.ds(pl.multiple_of(plane * PS + put, 8), count)
                land[:, own_rows] = fields[u, :, pl.ds(pl.multiple_of(o * R, 8), R)]
                continue
            to_t, to_s = place(u, jnp.clip(to, 0, bands - 1))
            send(
                source,
                lying(plane, put, count),
                s2.at[m, kind],
                r2.at[plane, kind],
                to_t,
                to_s,
                valid=valid,
                maybe_self=kind > 0 and q > 1,
            )

    for m in range(1, S):
        theirs = (s ^ m) * zl
        block_c = kin.at[0, pl.ds(theirs + share, half), k_to]
        block_v = kin.at[pl.ds(1, 3), pl.ds(theirs + share, half), k_to]
        arrived(block_c, rk.at[m, 0])
        arrived(block_v, rk.at[m, 1])
        send(block_c, block_c, sf.at[m, 0], rf.at[m, 0], partner, s)
        send(block_v, block_v, sf.at[m, 1], rf.at[m, 1], partner, s)
    for m in range(1, S):
        theirs = (s ^ m) * zl
        arrived(kin.at[0, pl.ds(theirs + rest, half), k_to], rf.at[m, 0])
        arrived(kin.at[pl.ds(1, 3), pl.ds(theirs + rest, half), k_to], rf.at[m, 1])

    angles = [2.0 * math.pi * u / U / 2 for u in range(U)]
    shift_re1 = by_index(unit, [rho * math.cos(a) for a in angles])
    shift_im1 = by_index(unit, [0.0] + [rho * math.sin(a) for a in angles[1:]])
    shift_re2 = by_index(unit, [-rho] + [rho * math.cos(a) for a in angles[1:]])
    z_at = lax.broadcasted_iota(jnp.int32, (NZ, NX), 0)
    x_at = lax.broadcasted_iota(jnp.int32, (NZ, NX), 1)

    def line(y):
        if isinstance(y, int):
            return pl.ds((y + O) * NZ, NZ)
        return pl.ds(pl.multiple_of((y + O) * NZ, 8), NZ)

    flat_kin = kin.reshape(4, NZ * PK, NX)

    @pl.loop(0, RH, unroll=4)
    def _(i):
        c, vz, vy, vx = [flat_kin[m, pl.ds(i + HALO, NZ, stride=PK)] for m in range(4)]
        to = line(i - HALO)
        az = c * vz
        ay = c * vy
        ax = c * vx
        zero = jnp.zeros_like(c)
        coef[0, to] = jnp.where(z_at == NZ - 1, zero, c - az)
        coef[1, to] = jnp.where(z_at == 0, zero, c + az)
        coef[2, to] = c - ay
        coef[3, to] = c + ay
        coef[4, to] = jnp.where(x_at == NX - 1, zero, c - ax)
        coef[5, to] = jnp.where(x_at == 0, zero, c + ax)
        diag1 = 1.0 + 6.0 * c - shift_re1
        diag2 = 1.0 + 6.0 * c - shift_re2
        im2 = shift_im1 * shift_im1
        modulus1 = diag1 * diag1 + im2
        modulus2 = diag2 * diag2 + im2
        pq[0, to] = diag1 / modulus1
        pq[1, to] = diag2 / modulus2
        pq[2, to] = shift_im1 / modulus1

    @pl.when(band == 0)
    def _():
        for z in range(NZ):
            land[:, z * PS : z * PS + HALO] = jnp.zeros((2, HALO, NX), jnp.float32)
        last[: HALO * NZ] = jnp.zeros((HALO * NZ, NX), jnp.float32)

    @pl.when(band == bands - 1)
    def _():
        for z in range(NZ):
            land[:, z * PS + HALO + R : z * PS + RH] = jnp.zeros((2, HALO, NX), jnp.float32)
        last[(HALO + R) * NZ :] = jnp.zeros((HALO * NZ, NX), jnp.float32)

    reach = -(-GUARD // R)
    counts = [min(R, GUARD - j * R) for j in range(reach)]
    for j in range(reach):
        spread = counts[j] * NZ

        @pl.when(band < j + 1)
        def _(j=j, spread=spread):
            first = (O - j * R - counts[j]) * NZ
            wc[:, first : first + spread] = jnp.zeros((2, spread, NX), jnp.float32)

        @pl.when(band + j + 1 > bands - 1)
        def _(j=j, spread=spread):
            first = (O + R + j * R) * NZ
            wc[:, first : first + spread] = jnp.zeros((2, spread, NX), jnp.float32)

    for m in range(NZ):
        z = plane ^ m
        if m:
            arrived(lying(z, HALO, R), r2.at[z, 0])
        arrived(lying(z, HALO + R, HALO), r2.at[z, 1], valid=band < bands - 1)
        arrived(lying(z, 0, HALO), r2.at[z, 2], valid=band > 0)

    def scaled(y, re_part, im_part):
        p1, p2, im = pq[0, line(y)], pq[1, line(y)], pq[2, line(y)]
        return re_part * p1 + im_part * im, im_part * p2 - re_part * im

    def neighbours(old, y, p):
        here = old[p, line(y)]
        total = src[p, line(y)] + coef[2, line(y)] * old[p, line(y + 1)] + coef[3, line(y)] * old[p, line(y - 1)]
        total += coef[0, line(y)] * shifted(here, -1, 0) + coef[1, line(y)] * shifted(here, 1, 0)
        total += coef[4, line(y)] * shifted(here, -1, 1) + coef[5, line(y)] * shifted(here, 1, 1)
        return total

    def sweep(old, new, low, high):
        for y in range(low, high):
            re_part, im_part = scaled(y, neighbours(old, y, 0), neighbours(old, y, 1))
            new[0, line(y)] = re_part
            new[1, line(y)] = im_part

    for y in range(-HALO, R + HALO):
        pair = [land[p, pl.ds(y + HALO, NZ, stride=PS)] for p in range(2)]
        src[0, line(y)] = pair[0]
        src[1, line(y)] = pair[1]
        re_part, im_part = scaled(y, *pair)
        wa[0, line(y)] = re_part
        wa[1, line(y)] = im_part
    old, new = wa, wb
    for k in range(1, SWEEPS):
        sweep(old, new, k - HALO, R + HALO - k)
        old, new = new, old
    weight = [2.0 * math.cos(2.0 * math.pi * u * (T - 1) / T) / T for u in range(U)]
    weight[0] = 1.0 / T
    other = [-2.0 * math.sin(2.0 * math.pi * u * (T - 1) / T) / T for u in range(U)]
    other[0] = (1.0 - 2.0 * ((T - 1) % 2)) / T
    weight_re = by_index(unit, [rho * w for w in weight])
    weight_im = by_index(unit, [rho * w for w in other])
    for y in range(R):
        re_part, im_part = scaled(y, neighbours(old, y, 0), neighbours(old, y, 1))
        wc[0, line(y)] = re_part
        wc[1, line(y)] = im_part
        part[y * NZ : y * NZ + NZ] = weight_re * re_part + weight_im * im_part

    def piece(u):
        return pl.ds(pl.multiple_of(u * chunk_rows, 8), chunk_rows)

    for m in range(U - 1, 0, -1):
        u = unit ^ m
        send(part.at[piece(u)], gathered.at[m], ss.at[m], rs.at[m], *place(u, band))

    def span(first, count):
        return pl.ds((first + O) * NZ, count * NZ)

    for j in range(reach):
        count = counts[j]
        above = jnp.minimum(band + j + 1, bands - 1)
        below = jnp.maximum(band - j - 1, 0)
        to_above = wc.at[:, span(-j * R - count, count)]
        to_below = wc.at[:, span(R + j * R, count)]
        source = wc.at[:, span(R - count, count)]
        send(source, to_above, sw.at[j, 0], rw.at[j, 0], *place(unit, above), valid=band + j + 1 < bands)
        source = wc.at[:, span(0, count)]
        send(source, to_below, sw.at[j, 1], rw.at[j, 1], *place(unit, below), valid=band >= j + 1)
    earlier = list(sent)
    sent.clear()
    for m in range(1, U):
        arrived(gathered.at[m], rs.at[m])
    total = part[piece(unit)]
    for m in range(1, U):
        total = total + gathered[m]
    reduced[...] = total
    base = HALO * NZ
    mine = pl.ds(pl.multiple_of(base + unit * chunk_rows, 8), chunk_rows)
    last[mine] = total
    low_at = pl.ds(pl.multiple_of((HALO + R) * NZ + jnp.minimum(unit, edges - 1) * chunk_rows, 8), chunk_rows)
    high_at = pl.ds(pl.multiple_of(jnp.maximum(unit - (U - edges), 0) * chunk_rows, 8), chunk_rows)
    goes_down = jnp.logical_and(band > 0, unit < edges)
    goes_up = jnp.logical_and(band < bands - 1, unit >= U - edges)
    for m in range(U - 1, -1, -1):
        u = unit ^ m
        below = place(u, jnp.maximum(band - 1, 0))
        above = place(u, jnp.minimum(band + 1, bands - 1))
        send(reduced, last.at[low_at], sg.at[m, 1], rg.at[m, 1], *below, valid=goes_down)
        send(reduced, last.at[high_at], sg.at[m, 2], rg.at[m, 2], *above, valid=goes_up)
        if m:
            send(reduced, last.at[mine], sg.at[m, 0], rg.at[m, 0], *place(u, band))
    for j in range(reach):
        count = counts[j]
        arrived(wc.at[:, span(-j * R - count, count)], rw.at[j, 0], valid=band >= j + 1)
        arrived(wc.at[:, span(R + j * R, count)], rw.at[j, 1], valid=band + j + 1 < bands)
    for y in range(-HALO, R + HALO):
        wa[0, line(y)] = neighbours(wc, y, 0)
        wa[1, line(y)] = neighbours(wc, y, 1)
    for finish in earlier:
        finish()
    for m in range(U):
        u = unit ^ m
        if m:
            arrived(last.at[pl.ds(pl.multiple_of(base + u * chunk_rows, 8), chunk_rows)], rg.at[m, 0])
        here = pl.ds(pl.multiple_of((HALO + R) * NZ + jnp.minimum(u, edges - 1) * chunk_rows, 8), chunk_rows)
        arrived(last.at[here], rg.at[m, 1], valid=jnp.logical_and(band < bands - 1, u < edges))
        here = pl.ds(pl.multiple_of(jnp.maximum(u - (U - edges), 0) * chunk_rows, 8), chunk_rows)
        arrived(last.at[here], rg.at[m, 2], valid=jnp.logical_and(band > 0, u >= U - edges))

    both = jnp.where(unit == 0, jnp.float32(1.0), jnp.float32(0.0))
    for y in range(-HALO, R + HALO):
        wrap = last[(y + HALO) * NZ : (y + HALO + 1) * NZ]
        wrap_im = wrap * both
        src[0, line(y)] = src[0, line(y)] - wrap
        src[1, line(y)] = src[1, line(y)] - wrap_im
        re_part, im_part = scaled(y, wa[0, line(y)] - wrap, wa[1, line(y)] - wrap_im)
        wb[0, line(y)] = re_part
        wb[1, line(y)] = im_part
    old, new = wb, wa
    for k in range(2, SWEEPS + 1):
        sweep(old, new, k - GUARD, R + GUARD - k)
        old, new = new, old
    for y in range(R):
        re_part, im_part = scaled(y, neighbours(old, y, 0), neighbours(old, y, 1))
        fin[0, pl.ds(y, NZ, stride=PF)] = re_part
        fin[1, pl.ds(y, NZ, stride=PF)] = im_part

    offset = pl.multiple_of((band % q) * R, 8)
    for m in range(NZ - 1, -1, -1):
        z = plane ^ m
        source = pl.ds(pl.multiple_of(z * PF, 8), R)
        if m == 0:
            back[pl.ds(unit, 1), :, pl.ds(offset, R)] = fin[:, source][None]
            continue
        send(
            fin.at[:, source],
            back.at[unit, :, pl.ds(offset, R)],
            s3.at[m],
            r3.at[unit, band % q],
            group * zl + z % zl,
            z // zl,
        )
    for m in range(1, U * q):
        spot = at ^ m
        u = spot // q
        o = spot % q
        arrived(back.at[u, :, pl.ds(pl.multiple_of(o * R, 8), R)], r3.at[u, o])
    for block in range(C // 8):
        rows = slice(block * 8, block * 8 + 8)
        result = inverse_transform([(back[u, 0, rows], back[u, 1, rows]) for u in range(U)], middle[rows])
        for m in range(T):
            states[m, rows] = result[m]
    for m in range(T - 1, 0, -1):
        tt = t ^ m
        send(states.at[tt], out_ref.at[chunk(t)], s4.at[m], r4.at[m], tt, s)
    out_ref[chunk(t)] = states[pl.ds(t, 1)][0]
    for finish in sent:
        finish()
    for m in range(1, T):
        arrived(out_ref.at[chunk(t ^ m)], r4.at[m])


def body(forcing, initial, coupling, velocity):
    local_steps, zl, NY, NX = forcing.shape
    T = lax.axis_size("tm")
    S = lax.axis_size("space")
    U = T // 2
    NZ = zl * S
    C = zl * NY // T
    bands = 2 * S
    R = NY // bands
    RH = R + 2 * HALO
    WC = C + 2 * HALO
    q = C // R
    PK = RH + 3 * HALO
    PS = RH + HALO
    PF = R + HALO
    rows = R + 2 * GUARD
    reach = -(-GUARD // R)
    assert local_steps == 1 and SWEEPS == HALO <= R and ITERS == 2
    assert S % q == 0 and zl % 2 == 0 and T % 4 == 0
    assert C % R == 0 and NY % C == 0 and U * q == NZ and NZ % 8 == 0
    assert T & (T - 1) == 0 and S & (S - 1) == 0 and NZ & (NZ - 1) == 0
    assert (R * NZ // U) % 8 == 0 and (HALO * U) % R == 0 and WC <= NY
    f32 = jnp.float32
    dma = pltpu.SemaphoreType.DMA
    hbm = pl.BlockSpec(memory_space=pltpu.HBM)
    out = pl.pallas_call(
        lambda *refs: kernel((T, S, NY, NX, zl), *refs),
        out_shape=jax.ShapeDtypeStruct((zl * NY, NX), f32),
        in_specs=[hbm] * 4,
        out_specs=pl.BlockSpec(memory_space=pltpu.VMEM),
        scratch_shapes=[
            pltpu.VMEM((zl * NY, NX), f32),
            pltpu.VMEM((zl, WC + 2 * HALO, NX), f32),
            pltpu.VMEM((4, C, NX), f32),
            pltpu.VMEM((T, C, NX), f32),
            pltpu.VMEM((U, 2, C, NX), f32),
            pltpu.VMEM((2, C, NX), f32),
            pltpu.VMEM((4, NZ, PK, NX), f32),
            pltpu.VMEM((6, rows * NZ, NX), f32),
            pltpu.VMEM((3, rows * NZ, NX), f32),
            pltpu.VMEM((2, NZ * PS, NX), f32),
            pltpu.VMEM((2, rows * NZ, NX), f32),
            pltpu.VMEM((2, rows * NZ, NX), f32),
            pltpu.VMEM((2, rows * NZ, NX), f32),
            pltpu.VMEM((2, rows * NZ, NX), f32),
            pltpu.VMEM((R * NZ, NX), f32),
            pltpu.VMEM((U, R * NZ // U, NX), f32),
            pltpu.VMEM((R * NZ // U, NX), f32),
            pltpu.VMEM((RH * NZ, NX), f32),
            pltpu.VMEM((2, NZ * PF, NX), f32),
            pltpu.VMEM((U, 2, C, NX), f32),
            pltpu.VMEM((T, C, NX), f32),
            dma((6,)),
            dma((T,)),
            dma((T,)),
            dma((NZ, 3)),
            dma((NZ, 3)),
            dma((S, 2)),
            dma((S, 2)),
            dma((S, 2)),
            dma((S, 2)),
            dma((2,)),
            dma((2,)),
            dma((reach, 2)),
            dma((reach, 2)),
            dma((U,)),
            dma((U,)),
            dma((U, 3)),
            dma((U, 3)),
            dma((NZ,)),
            dma((U, q)),
            dma((T,)),
            dma((T,)),
        ],
        compiler_params=pltpu.CompilerParams(
            has_side_effects=True, collective_id=0, vmem_limit_bytes=48 * 1024 * 1024
        ),
    )(forcing.reshape(zl * NY, NX), initial, coupling, velocity)
    return out.reshape(forcing.shape)


def solution(mesh):
    return jax.shard_map(
        body,
        mesh=mesh,
        in_specs=(
            P("tm", "space", None, None),
            P("space", None, None),
            P("space", None, None),
            P(None, "space", None, None),
        ),
        out_specs=P("tm", "space", None, None),
        check_vma=False,
    )
```

time: 47.3 us -> 48.9 us (1.034); the launches traced: 47.1 us -> 48.1 us
  local copies, waits for them, and re-layouts: 0.71 us -> 4.69 us
  Pallas kernels: 45 us -> 43.4 us
  other arithmetic: 1.42 us -> 0 us
    unnamed x3 -> x9, local copies, waits for them, and re-layouts: 0.71 us -> 4.69 us
    pallas_call x1, Pallas kernels: 45 us -> 43.4 us  [body(): pl.pallas_call(lambda *refs: kernel((T, S, NY, NX, zl), *refs), out_shape...]
    concatenate x1 -> x0, other arithmetic: 1.42 us -> none  [body(): stacked = jnp.concatenate([coupling[None], velocity, initial[None]], axis=0)]
where the time goes in v1:
time: 48.9 us; the launch traced here: 48.1 us
  Pallas kernels  43.4 us (89%)
  local copies, waits for them, and re-layouts  4.69 us (10%)
    pallas_call x1, Pallas kernels, body(): pl.pallas_call(lambda *refs: kernel((T, S, NY, NX, zl), *refs), out_shape...  43.4 us
    unnamed x9, local copies, waits for them, and re-layouts  4.69 us

profile of v1, /device:TPU:1, one launch (start us, length us, event | category | flops | bytes accessed | tf_op | source)
XLA Modules:
  0.0 48.1 jit_solution(15588128242521144870)
XLA Ops:
  0.0 0.0 copy-start
  0.0 1.1 %copy-done = f32[3,4,128,128]{3,2,1,0:T(8,128)S(1)} copy-done((f32[3,4,128,128]{3,2,1,0:T(8,128)S(1)}, f32[3,4,128,128]{3,2,1,0:T(8,128)}, u32[]{:S(2)}) %copy-start) | copy-done | bytes 786456
  1.1 0.0 copy-start.1
  1.1 0.9 %copy-done.1 = f32[1,4,128,128]{3,2,1,0:T(8,128)S(1)} copy-done((f32[1,4,128,128]{3,2,1,0:T(8,128)S(1)}, f32[1,4,128,128]{3,2,1,0:T(8,128)}, u32[]{:S(2)}) %copy-start.1) | copy-done | bytes 262168
  2.1 0.0 copy-start.2
  2.1 0.9 %copy-done.2 = f32[4,128,128]{2,1,0:T(8,128)S(1)} copy-done((f32[4,128,128]{2,1,0:T(8,128)S(1)}, f32[4,128,128]{2,1,0:T(8,128)}, u32[]{:S(2)}) %copy-start.2) | copy-done | bytes 262168
  3.0 0.0 copy-start.3
  3.0 0.9 %copy-done.3 = f32[4,128,128]{2,1,0:T(8,128)S(1)} copy-done((f32[4,128,128]{2,1,0:T(8,128)S(1)}, f32[4,128,128]{2,1,0:T(8,128)}, u32[]{:S(2)}) %copy-start.3) | copy-done | bytes 262168
  4.0 43.4 %shard_map.46 = f32[512,128]{1,0:T(8,128)S(1)} custom-call(f32[512,128]{1,0:T(8,128)S(1)} %bitcast.3, f32[4,128,128]{2,1,0:T(8,128)S(1)} %copy-done.2, f32[4,128,128]{2,1,0:T(8,128)S(1)} %copy-done.3, f32[3,4,128,128]{3,2,1,0:T(8,128)S(1)} %copy-done), custom_call_target="tpu_custom_call" | custom-call | tf_op jit(solution)/shard_map/pallas_call | solution.py:655
  47.4 0.7 %copy.6 = f32[1,4,128,128]{3,2,1,0:T(8,128)} copy(f32[1,4,128,128]{3,2,1,0:T(8,128)S(1)} %bitcast.2) | data formatting | bytes 524288
Async XLA Ops:
  0.0 1.1 %copy-start = (f32[3,4,128,128]{3,2,1,0:T(8,128)S(1)}, f32[3,4,128,128]{3,2,1,0:T(8,128)}, u32[]{:S(2)}) copy-start(f32[3,4,128,128]{3,2,1,0:T(8,128)} %refs_3_.1) | copy-start | bytes 2359300
  1.1 0.9 %copy-start.1 = (f32[1,4,128,128]{3,2,1,0:T(8,128)S(1)}, f32[1,4,128,128]{3,2,1,0:T(8,128)}, u32[]{:S(2)}) copy-start(f32[1,4,128,128]{3,2,1,0:T(8,128)} %param.4) | copy-start | bytes 786436
  2.1 0.9 %copy-start.2 = (f32[4,128,128]{2,1,0:T(8,128)S(1)}, f32[4,128,128]{2,1,0:T(8,128)}, u32[]{:S(2)}) copy-start(f32[4,128,128]{2,1,0:T(8,128)} %refs_1_.1) | copy-start | bytes 786436
  3.0 0.9 %copy-start.3 = (f32[4,128,128]{2,1,0:T(8,128)S(1)}, f32[4,128,128]{2,1,0:T(8,128)}, u32[]{:S(2)}) copy-start(f32[4,128,128]{2,1,0:T(8,128)} %refs_2_.1) | copy-start | bytes 786436

commit v2 on v1

--- a/solution.py
+++ b/solution.py
@@ -363,12 +363,12 @@
     def lying(z, first, count):
         return land.at[:, pl.ds(pl.multiple_of(z * PS + first, 8), count)]
 
-    for m in range(NZ - 1, -1, -1):
+    for kind, m in [(0, m) for m in range(NZ - 1, -1, -1)] + [(k, m) for m in range(NZ - 1, -1, -1) for k in (1, 2)]:
         spot = at ^ m
         u = spot // q
         o = spot % q
         b = group * q + o
-        for kind in range(3):
+        if True:
             to = b + (0, -1, 1)[kind]
             valid = (None, to >= 0, to < bands)[kind]
             first, count, put = kinds[kind]
@@ -617,14 +617,14 @@
         result = inverse_transform([(back[u, 0, rows], back[u, 1, rows]) for u in range(U)], middle[rows])
         for m in range(T):
             states[m, rows] = result[m]
-    for m in range(T - 1, 0, -1):
-        tt = t ^ m
+    for m in range(1, T):
+        tt = lax.rem(t + m, T)
         send(states.at[tt], out_ref.at[chunk(t)], s4.at[m], r4.at[m], tt, s)
     out_ref[chunk(t)] = states[pl.ds(t, 1)][0]
     for finish in sent:
         finish()
     for m in range(1, T):
-        arrived(out_ref.at[chunk(t ^ m)], r4.at[m])
+        arrived(out_ref.at[chunk(lax.rem(t + T - m, T))], r4.at[m])
 
 
 def body(forcing, initial, coupling, velocity):
@@ -704,7 +704,7 @@
         compiler_params=pltpu.CompilerParams(
             has_side_effects=True, collective_id=0, vmem_limit_bytes=48 * 1024 * 1024
         ),
-    )(forcing.reshape(zl * NY, NX), initial, coupling, velocity)
+    )(*[pltpu.with_memory_space_constraint(a, pltpu.HBM) for a in (forcing.reshape(zl * NY, NX), initial, coupling, velocity)])
     return out.reshape(forcing.shape)
 
 

time: 48.9 us -> 42.6 us (0.87); the launches traced: 48.1 us -> 42.5 us
  local copies, waits for them, and re-layouts: 4.69 us -> 0.71 us
  Pallas kernels: 43.4 us -> 41.8 us
    unnamed x9 -> x1, local copies, waits for them, and re-layouts: 4.69 us -> 0.71 us
    pallas_call x1, Pallas kernels: 43.4 us -> 41.8 us  [body(): pl.pallas_call(lambda *refs: kernel((T, S, NY, NX, zl), *refs), out_shape...]
where the time goes in v2:
time: 42.6 us; the launch traced here: 42.5 us
  Pallas kernels  41.8 us (98%)
  local copies, waits for them, and re-layouts  0.71 us (2%)
    pallas_call x1, Pallas kernels, body(): pl.pallas_call(lambda *refs: kernel((T, S, NY, NX, zl), *refs), out_shape...  41.8 us

profile of v2, /device:TPU:1, one launch (start us, length us, event | category | flops | bytes accessed | tf_op | source)
XLA Modules:
  0.0 42.5 jit_solution(17292475357628995546)
XLA Ops:
  0.0 41.8 %shard_map.46 = f32[512,128]{1,0:T(8,128)S(1)} custom-call(f32[512,128]{1,0:T(8,128)} %bitcast.3, f32[4,128,128]{2,1,0:T(8,128)} %refs_1_.1, f32[4,128,128]{2,1,0:T(8,128)} %refs_2_.1, f32[3,4,128,128]{3,2,1,0:T(8,128)} %refs_3_.1), custom_call_target="tpu_custom_call" | custom-call | tf_op jit(solution)/shard_map/pallas_call | solution.py:655
  41.8 0.7 %copy.6 = f32[1,4,128,128]{3,2,1,0:T(8,128)} copy(f32[1,4,128,128]{3,2,1,0:T(8,128)S(1)} %bitcast.2) | data formatting | bytes 524288
